TPU v7x, 32 devices: a whole 2x2x4 slice. The times are simulated.
32 devices in a mesh: dp: 8 (over z, x), tp: 4 (over y, core).
Axes of the slice: x: 2, y: 2, z: 4, core: 2. Of those that a mesh axis runs over, the one named last changes fastest.
Arguments:
- main: bfloat16 [16512, 1152], P('dp', 'tp'), may hold values from -6 to 6
- long_skip: bfloat16 [16512, 1152], P('dp', 'tp'), may hold values from -6 to 6
- cotangent: bfloat16 [16512, 1152], P('dp', 'tp'), may hold values from -6 to 6
- timesteps: int32 [64], P('dp'), may hold values from 0 to 999
- loss_codes: int32 [64], P('dp'), may hold values from 0 to 7
- code_weights: float32 [8], replicated, may hold values from 0.25 to 4
- item_counts: int32 [8], P('dp'), may hold values from 4 to 8, as said below
- w_skip_main: bfloat16 [1152, 1152], P('tp'), may hold values from -0.125 to 0.125
- w_skip_long: bfloat16 [1152, 1152], P('tp'), may hold values from -0.125 to 0.125
- b_skip: float32 [1152], P('tp'), may hold values from -3 to 3
- ln1_gain: float32 [1152], P('tp'), may hold values from 0.25 to 1.75
- ln1_bias: float32 [1152], P('tp'), may hold values from -2.4 to 2.4
- w_qkv: bfloat16 [3, 1152, 1152], P(None, None, 'tp'), may hold values from -0.1875 to 0.1875
- w_proj: bfloat16 [1152, 1152], P('tp'), may hold values from -1.5 to 1.5
- b_proj: float32 [1152], P('tp'), may hold values from -3 to 3
- ln2_gain: float32 [1152], P('tp'), may hold values from 0.25 to 1.75
- ln2_bias: float32 [1152], P('tp'), may hold values from -2.4 to 2.4
- w_up: bfloat16 [1152, 4608], P(None, 'tp'), may hold values from -0.1875 to 0.1875
- b_up: float32 [4608], P('tp'), may hold values from -3 to 3
- w_down: bfloat16 [4608, 1152], P('tp'), may hold values from -0.09375 to 0.09375
- b_down: float32 [1152], P('tp'), may hold values from -3 to 3
Outputs:
- out: bfloat16 [16512, 1152], P('dp', 'tp')
- d_main: bfloat16 [16512, 1152], P('dp', 'tp')
- d_long: bfloat16 [16512, 1152], P('dp', 'tp')
- g_w_skip_main: float32 [1152, 1152], P('tp')
- g_w_skip_long: float32 [1152, 1152], P('tp')
- g_b_skip: float32 [1152], P('tp')
- g_ln1_gain: float32 [1152], P('tp')
- g_ln1_bias: float32 [1152], P('tp')
- g_w_qkv: float32 [3, 1152, 1152], P(None, None, 'tp')
- g_w_proj: float32 [1152, 1152], P('tp')
- g_b_proj: float32 [1152], P('tp')
- g_ln2_gain: float32 [1152], P('tp')
- g_ln2_bias: float32 [1152], P('tp')
- g_w_up: float32 [1152, 4608], P(None, 'tp')
- g_b_up: float32 [4608], P('tp')
- g_w_down: float32 [4608, 1152], P('tp')
- g_b_down: float32 [1152], P('tp')
Inputs may be any that keep to these rules, and one draw needn't show every extreme that they name: `item_counts`: each batch group holds 4 to 8 items; some group is full and some holds exactly 4.
All inputs are finite; a program needn't handle non-finite values.
Results may differ from a plain program's by a relative error of at most 0.02.
Values may be sent and summed in bfloat16 or wider, within the bound.
A program may use at most 192 MiB of HBM per device.

v0:
```python
import math

import jax
import jax.numpy as jnp
from jax import lax
from jax.sharding import PartitionSpec as P

HEAD = 72
SEQ = 258
TSTEPS = 1000


EPSILON = 1e-06
ROOT_HALF = 0.7071067811865476
DENSITY_SCALE = 0.3989422804014327


def item_factors(timesteps, loss_codes, code_weights, group_items):
    steps_float = timesteps.astype(jnp.float32)
    phase = (steps_float / TSTEPS + 0.008) / 1.008 * (math.pi / 2.0)
    cosine = jnp.cos(phase)
    signal = cosine * cosine
    weight = jnp.minimum(1.0, 5.0 * (1.0 - signal) / signal)
    picks = (
        loss_codes[:, None] == jnp.arange(code_weights.shape[0], dtype=jnp.int32)[None, :]
    ).astype(jnp.float32)
    coded = jnp.sum(picks * code_weights[None, :], axis=1)
    valid = (jnp.arange(timesteps.shape[0], dtype=jnp.int32) < group_items).astype(jnp.float32)
    return (weight * coded * valid, valid)


def layer_norm(stream, gain, bias, width):
    totals, squares = lax.psum((jnp.sum(stream, 0), jnp.sum(stream * stream, 0)), "tp")
    mean = totals / width
    rstd = lax.rsqrt(squares / width - mean * mean + EPSILON)
    normed = (stream - mean[None, :]) * rstd[None, :]
    rounded = (normed * gain[:, None] + bias[:, None]).astype(jnp.bfloat16)
    return (normed, rstd, lax.all_gather(rounded, "tp", axis=0, tiled=True))


def norm_back(d_normed, normed, rstd, gain, width):
    g_gain = jnp.sum(d_normed * normed, 1)
    g_bias = jnp.sum(d_normed, 1)
    scaled = d_normed * gain[:, None]
    first, second = lax.psum((jnp.sum(scaled, 0), jnp.sum(scaled * normed, 0)), "tp")
    back = rstd[None, :] * (scaled - first[None, :] / width - normed * second[None, :] / width)
    return (back, g_gain, g_bias)


def reduce_back(term, local_width):
    return lax.psum_scatter(
        term(jnp.int32(0), lax.axis_size("tp") * local_width).astype(jnp.bfloat16),
        "tp",
        scatter_dimension=0,
        tiled=True,
    ).astype(jnp.float32)


def fold_back(shard, pairs):
    piece = lax.all_gather(shard, "tp", axis=0, tiled=True)
    new_acts = tuple(
        (
            jnp.einsum("fc,ct->ft", weight, piece, preferred_element_type=jnp.float32)
            for weight, acts in pairs
        )
    )
    new_weights = tuple(
        (
            jnp.einsum("ft,ct->fc", acts, piece, preferred_element_type=jnp.float32)
            for weight, acts in pairs
        )
    )
    return (new_acts, new_weights)


def split_heads(flat, heads_here):
    pair_count = flat.shape[1] // (2 * SEQ)
    shaped = flat.reshape(heads_here, HEAD, pair_count, 2, SEQ)
    return jnp.moveaxis(shaped, 2, 0)


def join_heads(blocks):
    moved = jnp.moveaxis(blocks, 0, 2)
    return moved.reshape(moved.shape[0] * moved.shape[1], -1)


def attend(block):
    query_rows, key_rows, value_rows = block
    scale = 1.0 / math.sqrt(HEAD)
    scores = (
        jnp.einsum("hdbi,hdbj->hbij", query_rows, key_rows, preferred_element_type=jnp.float32)
        * scale
    )
    peak = jnp.max(scores, axis=-1, keepdims=True)
    logsum = peak + jnp.log(jnp.sum(jnp.exp(scores - peak), axis=-1, keepdims=True))
    probs = jnp.exp(scores - logsum).astype(jnp.bfloat16)
    attended = jnp.einsum("hbij,hdbj->hdbi", probs, value_rows, preferred_element_type=jnp.float32)
    return (attended.astype(jnp.bfloat16), logsum[..., 0])


def attend_back(block):
    query_rows, key_rows, value_rows, logsum, d_attended = block
    scale = 1.0 / math.sqrt(HEAD)
    scores = (
        jnp.einsum("hdbi,hdbj->hbij", query_rows, key_rows, preferred_element_type=jnp.float32)
        * scale
    )
    probs = jnp.exp(scores - logsum[..., None])
    probs_low = probs.astype(jnp.bfloat16)
    d_probs = jnp.einsum(
        "hdbi,hdbj->hbij", d_attended, value_rows, preferred_element_type=jnp.float32
    )
    delta = jnp.sum(probs * d_probs, axis=-1, keepdims=True)
    d_scores = (probs * (d_probs - delta)).astype(jnp.bfloat16)
    d_query = (
        jnp.einsum("hbij,hdbj->hdbi", d_scores, key_rows, preferred_element_type=jnp.float32)
        * scale
    )
    d_key = (
        jnp.einsum("hbij,hdbi->hdbj", d_scores, query_rows, preferred_element_type=jnp.float32)
        * scale
    )
    d_value = jnp.einsum(
        "hbij,hdbi->hdbj", probs_low, d_attended, preferred_element_type=jnp.float32
    )
    return (d_query.astype(jnp.bfloat16), d_key.astype(jnp.bfloat16), d_value.astype(jnp.bfloat16))


def body(
    main,
    long_skip,
    cotangent,
    timesteps,
    loss_codes,
    code_weights,
    item_counts,
    w_skip_main,
    w_skip_long,
    b_skip,
    ln1_gain,
    ln1_bias,
    w_qkv,
    w_proj,
    b_proj,
    ln2_gain,
    ln2_bias,
    w_up,
    b_up,
    w_down,
    b_down,
):
    local_width = main.shape[1]
    width = w_skip_main.shape[1]
    heads_here = local_width // HEAD
    item_scale, valid = item_factors(timesteps, loss_codes, code_weights, item_counts[0])
    row_scale = jnp.repeat(item_scale, SEQ)
    row_valid = jnp.repeat(valid, SEQ)
    main_cols = main.T
    long_cols = long_skip.T
    stream = (
        lax.psum_scatter(
            jnp.einsum("dc,dt->ct", w_skip_main, main_cols, preferred_element_type=jnp.float32)
            + jnp.einsum("dc,dt->ct", w_skip_long, long_cols, preferred_element_type=jnp.float32),
            "tp",
            scatter_dimension=0,
            tiled=True,
        )
        + b_skip[:, None]
    )
    normed_one, rstd_one, full_one = layer_norm(stream, ln1_gain, ln1_bias, width)
    qkv = jnp.einsum("edc,dt->ect", w_qkv, full_one, preferred_element_type=jnp.float32).astype(
        jnp.bfloat16
    )
    query_blocks = split_heads(qkv[0], heads_here)
    key_blocks = split_heads(qkv[1], heads_here)
    value_blocks = split_heads(qkv[2], heads_here)
    attended_blocks, logsums = lax.map(attend, (query_blocks, key_blocks, value_blocks))
    attended = join_heads(attended_blocks)
    cols_here = w_proj
    projected = lax.psum_scatter(
        jnp.einsum("rc,rt->ct", cols_here, attended, preferred_element_type=jnp.float32).astype(
            jnp.bfloat16
        ),
        "tp",
        scatter_dimension=0,
        tiled=True,
    ).astype(jnp.float32)
    stream_two = stream + projected + b_proj[:, None]
    normed_two, rstd_two, full_two = layer_norm(stream_two, ln2_gain, ln2_bias, width)
    upward = (
        jnp.einsum("dc,dt->ct", w_up, full_two, preferred_element_type=jnp.float32) + b_up[:, None]
    )
    activated = jax.nn.gelu(upward, approximate=False).astype(jnp.bfloat16)
    cols_here = w_down
    result = (
        stream_two
        + lax.psum_scatter(
            jnp.einsum(
                "fc,ft->ct", cols_here, activated, preferred_element_type=jnp.float32
            ).astype(jnp.bfloat16),
            "tp",
            scatter_dimension=0,
            tiled=True,
        ).astype(jnp.float32)
        + b_down[:, None]
    )
    out = (result * row_valid[None, :]).T.astype(jnp.bfloat16)
    grad_low = (cotangent.T.astype(jnp.float32) * row_scale[None, :]).astype(jnp.bfloat16)
    grad_wide = grad_low.astype(jnp.float32)
    g_b_down = jnp.sum(grad_wide, 1)
    (d_activated,), (g_w_down,) = fold_back(grad_low, ((w_down, activated),))
    cumulative = 0.5 * (1.0 + lax.erf(upward * ROOT_HALF))
    density = jnp.exp(-0.5 * upward * upward) * DENSITY_SCALE
    d_upward = (d_activated * (cumulative + upward * density)).astype(jnp.bfloat16)
    g_b_up = jnp.sum(d_upward.astype(jnp.float32), 1)
    g_w_up = jnp.einsum("dt,ft->df", full_two, d_upward, preferred_element_type=jnp.float32)

    def up_term(start, count_rows):
        return jnp.einsum("cf,ft->ct", w_up, d_upward, preferred_element_type=jnp.float32)

    d_normed_two = reduce_back(up_term, local_width)
    back_two, g_ln2_gain, g_ln2_bias = norm_back(
        d_normed_two, normed_two, rstd_two, ln2_gain, width
    )
    d_stream_two = (back_two + grad_wide).astype(jnp.bfloat16)
    d_stream_wide = d_stream_two.astype(jnp.float32)
    g_b_proj = jnp.sum(d_stream_wide, 1)
    (d_attended,), (g_w_proj,) = fold_back(d_stream_two, ((w_proj, attended),))
    d_attended_blocks = split_heads(d_attended.astype(jnp.bfloat16), heads_here)
    d_queries, d_keys, d_values = lax.map(
        attend_back, (query_blocks, key_blocks, value_blocks, logsums, d_attended_blocks)
    )
    d_qkv = jnp.stack([join_heads(d_queries), join_heads(d_keys), join_heads(d_values)], axis=0)
    g_w_qkv = jnp.einsum("dt,ect->edc", full_one, d_qkv, preferred_element_type=jnp.float32)

    def qkv_term(start, count_rows):
        return jnp.einsum("ecr,ert->ct", w_qkv, d_qkv, preferred_element_type=jnp.float32)

    d_normed_one = reduce_back(qkv_term, local_width)
    back_one, g_ln1_gain, g_ln1_bias = norm_back(
        d_normed_one, normed_one, rstd_one, ln1_gain, width
    )
    d_stream = (back_one + d_stream_wide).astype(jnp.bfloat16)
    g_b_skip = jnp.sum(d_stream.astype(jnp.float32), 1)
    (d_main_cols, d_long_cols), (g_w_main, g_w_long) = fold_back(
        d_stream, ((w_skip_main, main_cols), (w_skip_long, long_cols))
    )
    (
        g_w_main,
        g_w_long,
        g_b_skip,
        g_ln1_gain,
        g_ln1_bias,
        g_w_qkv,
        g_w_proj,
        g_b_proj,
        g_ln2_gain,
        g_ln2_bias,
        g_w_up,
        g_b_up,
        g_w_down,
        g_b_down,
    ) = (
        lax.psum(g_w_main.astype(jnp.bfloat16), "dp").astype(jnp.float32),
        lax.psum(g_w_long.astype(jnp.bfloat16), "dp").astype(jnp.float32),
        lax.psum(g_b_skip.astype(jnp.bfloat16), "dp").astype(jnp.float32),
        lax.psum(g_ln1_gain.astype(jnp.bfloat16), "dp").astype(jnp.float32),
        lax.psum(g_ln1_bias.astype(jnp.bfloat16), "dp").astype(jnp.float32),
        lax.psum(g_w_qkv.astype(jnp.bfloat16), "dp").astype(jnp.float32),
        lax.psum(g_w_proj.astype(jnp.bfloat16), "dp").astype(jnp.float32),
        lax.psum(g_b_proj.astype(jnp.bfloat16), "dp").astype(jnp.float32),
        lax.psum(g_ln2_gain.astype(jnp.bfloat16), "dp").astype(jnp.float32),
        lax.psum(g_ln2_bias.astype(jnp.bfloat16), "dp").astype(jnp.float32),
        lax.psum(g_w_up.astype(jnp.bfloat16), "dp").astype(jnp.float32),
        lax.psum(g_b_up.astype(jnp.bfloat16), "dp").astype(jnp.float32),
        lax.psum(g_w_down.astype(jnp.bfloat16), "dp").astype(jnp.float32),
        lax.psum(g_b_down.astype(jnp.bfloat16), "dp").astype(jnp.float32),
    )
    d_main = d_main_cols.T.astype(jnp.bfloat16)
    d_long = d_long_cols.T.astype(jnp.bfloat16)
    return (
        out,
        d_main,
        d_long,
        g_w_main,
        g_w_long,
        g_b_skip,
        g_ln1_gain,
        g_ln1_bias,
        g_w_qkv,
        g_w_proj,
        g_b_proj,
        g_ln2_gain,
        g_ln2_bias,
        g_w_up,
        g_b_up,
        g_w_down,
        g_b_down,
    )


def solution(mesh):
    return jax.shard_map(
        body,
        mesh=mesh,
        in_specs=(
            P("dp", "tp"),
            P("dp", "tp"),
            P("dp", "tp"),
            P("dp"),
            P("dp"),
            P(),
            P("dp"),
            P("tp", None),
            P("tp", None),
            P("tp"),
            P("tp"),
            P("tp"),
            P(None, None, "tp"),
            P("tp", None),
            P("tp"),
            P("tp"),
            P("tp"),
            P(None, "tp"),
            P("tp"),
            P("tp", None),
            P("tp"),
        ),
        out_specs=(
            P("dp", "tp"),
            P("dp", "tp"),
            P("dp", "tp"),
            P("tp", None),
            P("tp", None),
            P("tp"),
            P("tp"),
            P("tp"),
            P(None, None, "tp"),
            P("tp", None),
            P("tp"),
            P("tp"),
            P("tp"),
            P(None, "tp"),
            P("tp"),
            P("tp", None),
            P("tp"),
        ),
        check_vma=False,
    )
```

profile of v0, /device:TPU:0, one launch (start us, length us, event | category | flops | bytes accessed | tf_op | source)
XLA Modules:
  0.0 1135.2 jit_solution(10548227006924629064)
XLA Ops:
  11.9 6.9 convolution_add_fusion
  18.9 84.4 %reduce-scatter.16.cloned.1.call-done = f32[288,2064]{1,0:T(8,128)} async-done(((f32[1152,2064]{1,0:T(8,128)}), f32[288,2064]{1,0:T(8,128)}) %reduce-scatter.16.cloned.1.call-update) | async-done | bytes 2377744
  109.4 10.3 all-reduce.3
  126.7 39.5 %all-gather.6.cloned.1.call-done = bf16[1152,2064]{1,0:T(8,128)(2,1)} async-done(((bf16[288,2064]{1,0:T(8,128)(2,1)}), bf16[1152,2064]{1,0:T(8,128)(2,1)}) %all-gather.6.cloned.1.call-update) | async-done | bytes 4755472 | tf_op jit(solution)/shard_map/all_gather | solution.py:38
  166.2 8.2 fusion.83
  176.4 6.6 reshape_squeeze.11
  183.0 6.6 reshape_squeeze.10
  203.0 23.4 %while.26 = (s32[]{:T(128)}, bf16[4,4,72,2,258]{4,2,3,1,0:T(8,128)(2,1)}, f32[4,4,2,258]{3,2,1,0:T(2,128)}, bf16[4,4,72,2,258]{4,2,3,1,0:T(8,128)(2,1)}, bf16[4,...) while((s32[]{:T(128)}, bf16[4,4,72,2,258]{4,2,3,1,0:T(8,128)(2,1)}, ...), condition=%wide.region_8.0_spmd, body=%wide.region_5.8_spmd.sunk | while | flops 157770096 | bytes 8231833 | solution.py:177
  242.0 8.4 copy.129
  250.5 50.0 %reduce-scatter.18.cloned.1.call-done = bf16[288,2064]{1,0:T(8,128)(2,1)} async-done(((bf16[1152,2064]{1,0:T(8,128)(2,1)}), bf16[288,2064]{1,0:T(8,128)(2,1)}) %reduce-scatter.18.cloned.1.call-update) | async-done | bytes 1188880
  307.6 10.3 all-reduce.2
  333.6 30.3 %all-gather.8.cloned.1.call-done = bf16[1152,2064]{1,0:T(8,128)(2,1)} async-done(((bf16[288,2064]{1,0:T(8,128)(2,1)}), bf16[1152,2064]{1,0:T(8,128)(2,1)}) %all-gather.8.cloned.1.call-update) | async-done | bytes 4755472 | tf_op jit(solution)/shard_map/all_gather | solution.py:38
  363.9 32.2 %fusion.68 = (bf16[1152,2064]{0,1:T(8,128)(2,1)S(1)}, f32[1152,2064]{0,1:T(8,128)}) fusion(f32[1152]{0:T(1024)S(1)} %copy-done.46, bf16[1152,2064]{1,0:T(8,128)(2,1)} %all-gather.8.cloned.1.call-done, bf16[1152,1152]{1,0:T(8,128)(2,1)S(1)} %copy-done), kind=kOutput, calls=%fused_computation.81 | convolution fusion | flops 5635215360 | bytes 21680640 | tf_op jit(solution)/shard_map/dc,dt->ct/dot_general | solution.py:191
  398.4 8.5 fusion.63
  406.9 8.4 copy.131
  415.3 16.6 %fusion.122 = (bf16[1152]{0:T(1024)(128)(2,1)}, bf16[1152,2064]{0,1:T(8,128)(2,1)S(1)}) fusion(f32[1152,2064]{0,1:T(8,128)} %get-tuple-element.220, bf16[1152,2064]{1,0:T(8,128)(2,1)} %all-gather.10.cloned.1.call-done, bf16[1152,1152]{1,0:T(8,128)(2,1)} %param.44), kind=kOutput, calls=%fused_computation.176 | convolution fusion | flops 5504439296 | bytes 21678336 | tf_op jit(solution)/shard_map/fc,ct->ft/dot_general | solution.py:63
  434.1 8.7 fusion.64
  442.8 8.4 copy.133
  451.4 13.8 %reduce-scatter.20.cloned.1.call-done = bf16[288,2064]{1,0:T(8,128)(2,1)} async-done(((bf16[1152,2064]{1,0:T(8,128)(2,1)}), bf16[288,2064]{1,0:T(8,128)(2,1)}) %reduce-scatter.20.cloned.1.call-update) | async-done | bytes 1188880
  467.8 50.5 %reduce-scatter.22.cloned.1.call-done = bf16[288,2064]{1,0:T(8,128)(2,1)} async-done(((bf16[1152,2064]{1,0:T(8,128)(2,1)}), bf16[288,2064]{1,0:T(8,128)(2,1)}) %reduce-scatter.22.cloned.1.call-update) | async-done | bytes 1188880
  526.9 10.3 all-reduce.1
  544.9 39.8 %all-gather.12.cloned.1.call-done = bf16[1152,2064]{1,0:T(8,128)(2,1)} async-done(((bf16[288,2064]{1,0:T(8,128)(2,1)}), bf16[1152,2064]{1,0:T(8,128)(2,1)}) %all-gather.12.cloned.1.call-update) | async-done | bytes 4755472 | tf_op jit(solution)/shard_map/all_gather | solution.py:60
  601.7 51.3 %while.27 = (s32[]{:T(128)}, bf16[4,4,72,2,258]{4,2,3,1,0:T(8,128)(2,1)}, bf16[4,4,72,2,258]{4,2,3,1,0:T(8,128)(2,1)}, bf16[4,4,72,2,258]{4,2,3,1,0:T(8,128)(2,1...) while((s32[]{:T(128)}, ...), condition=%wide.region_23.24_spmd, body=%wide.region_21.23_spmd.sunk | while | flops 390539744 | bytes 20462064 | solution.py:230
  678.8 7.7 fusion.65
  686.5 8.4 copy.135
  695.0 50.0 %reduce-scatter.24.cloned.1.call-done = bf16[288,2064]{1,0:T(8,128)(2,1)} async-done(((bf16[1152,2064]{1,0:T(8,128)(2,1)}), bf16[288,2064]{1,0:T(8,128)(2,1)}) %reduce-scatter.24.cloned.1.call-update) | async-done | bytes 1188880
  751.9 10.5 all-reduce
  770.1 11.5 %convolution_convert_fusion.4 = bf16[1152,1152]{1,0:T(8,128)(2,1)} fusion(bf16[1152,2064]{1,0:T(8,128)(2,1)} %all-gather.8.cloned.1.call-done, bf16[1152,2064]{0,1:T(8,128)(2,1)} %copy-done.49), kind=kOutput, calls=%fused_computation.102 | convolution fusion | flops 5479612416 | bytes 12165120 | tf_op jit(solution)/shard_map/dt,ft->df/dot_general | solution.py:216
  781.6 12.4 %convolution_convert_fusion.3 = bf16[1152,1152]{1,0:T(8,128)(2,1)} fusion(bf16[1152,2064]{0,1:T(8,128)(2,1)} %copy-done.50, bf16[1152,2064]{1,0:T(8,128)(2,1)} %all-gather.10.cloned.1.call-done), kind=kOutput, calls=%fused_computation.101 | convolution fusion | flops 5479612416 | bytes 12165120 | tf_op jit(solution)/shard_map/ft,ct->fc/dot_general | solution.py:69
  796.9 6.9 fusion.108
  823.3 39.2 %all-reduce.4 = (bf16[288]{0:T(512)(128)(2,1)S(1)}, bf16[288]{0:T(512)(128)(2,1)S(1)}, bf16[288]{0:T(512)(128)(2,1)S(1)}, bf16[288]{0:T(512)(128)(2,1)S(1)}, bf1...) all-reduce(bf16[288]{0:T(512)(128)(2,1)S(1)} %get-tuple-element.204, ...), channel_id=1, replica_groups=mesh['dp'=8,'tp'=4] {'dp'}, use_global_device_ids=true, to_apply=%region_32.33 | all-reduce | flops 3168 | bytes 12672 | tf_op jit(solution)/shard_map/psum | solution.py:266
  877.9 235.9 %all-reduce.8.cloned.1.call-done = (bf16[288,1152]{1,0:T(8,128)(2,1)}, bf16[288,1152]{1,0:T(8,128)(2,1)}, bf16[3,1152,288]{1,2,0:T(8,128)(2,1)}, bf16[288,1152]{...) async-done(((bf16[288,1152]{1,0:T(8,128)(2,1)}, bf16[288,1152]{1,0:T(8,128)(2,1)}, bf16[3,1152,288]{1,2,0:T(8,128)(2,1)}, ...) | async-done | bytes 9289744 | tf_op jit(solution)/shard_map/psum | solution.py:264
  (259 shorter events, 278.4 us)
Async XLA Ops:
  7.2 356.7 %copy-start = (bf16[1152,1152]{1,0:T(8,128)(2,1)S(1)}, bf16[1152,1152]{1,0:T(8,128)(2,1)}, u32[]{:S(2)}) copy-start(bf16[1152,1152]{1,0:T(8,128)(2,1)} %param.42) | copy-start | bytes 7962628
  7.2 96.1 %reduce-scatter.16.cloned.1.call-start = ((), (), s32[]{:S(2)}) async-start(), calls=%async_computation.10 | async-start | bytes 12533760
  18.8 88.0 %copy-start.30 = (f32[288]{0:T(512)S(1)}, f32[288]{0:T(512)}, u32[]{:S(2)}) copy-start(f32[288]{0:T(512)} %param.34) | copy-start | bytes 3460
  18.8 101.5 %copy-start.33 = (f32[288]{0:T(512)S(1)}, f32[288]{0:T(512)}, u32[]{:S(2)}) copy-start(f32[288]{0:T(512)} %param.35) | copy-start | bytes 3460
  18.9 101.5 %copy-start.36 = (f32[288]{0:T(512)S(1)}, f32[288]{0:T(512)}, u32[]{:S(2)}) copy-start(f32[288]{0:T(512)} %param.36) | copy-start | bytes 3460
  18.9 147.4 %all-gather.6.cloned.1.call-start = ((), (), s32[]{:S(2)}) async-start(), calls=%async_computation.5 | async-start | bytes 6266880 | tf_op jit(solution)/shard_map/all_gather | solution.py:38
  126.4 174.0 %reduce-scatter.18.cloned.1.call-start = ((), (), s32[]{:S(2)}) async-start(), calls=%async_computation.11 | async-start | bytes 6266880
  250.4 52.6 %copy-start.37 = (f32[288]{0:T(512)S(1)}, f32[288]{0:T(512)}, u32[]{:S(2)}) copy-start(f32[288]{0:T(512)} %param.39) | copy-start | bytes 3460
  250.4 113.5 %all-gather.8.cloned.1.call-start = ((), (), s32[]{:S(2)}) async-start(), calls=%async_computation.6 | async-start | bytes 6266880 | tf_op jit(solution)/shard_map/all_gather | solution.py:38
  303.0 14.9 %copy-start.32 = (f32[288]{0:T(512)S(1)}, f32[288]{0:T(512)}, u32[]{:S(2)}) copy-start(f32[288]{0:T(512)} %param.40) | copy-start | bytes 3460
  303.0 14.9 %copy-start.38 = (f32[288]{0:T(512)S(1)}, f32[288]{0:T(512)}, u32[]{:S(2)}) copy-start(f32[288]{0:T(512)} %param.41) | copy-start | bytes 3460
  324.0 91.3 %all-gather.10.cloned.1.call-start = ((), (), s32[]{:S(2)}) async-start(), calls=%async_computation.7 | async-start | bytes 6266880 | tf_op jit(solution)/shard_map/all_gather | solution.py:60
  328.0 35.9 %copy-start.46 = (f32[1152]{0:T(1024)S(1)}, f32[1152]{0:T(1024)}, u32[]{:S(2)}) copy-start(f32[1152]{0:T(1024)} %param.43) | copy-start | bytes 13828
  333.6 131.7 %reduce-scatter.20.cloned.1.call-start = ((), (), s32[]{:S(2)}) async-start(), calls=%async_computation.12 | async-start | bytes 6266880
  363.9 34.5 %copy-start.42 = (bf16[1152,1152]{1,0:T(8,128)(2,1)S(1)}, bf16[1152,1152]{1,0:T(8,128)(2,1)}, u32[]{:S(2)}) copy-start(bf16[1152,1152]{1,0:T(8,128)(2,1)} %param.44) | copy-start | bytes 7962628
  415.3 103.1 %reduce-scatter.22.cloned.1.call-start = ((), (), s32[]{:S(2)}) async-start(), calls=%async_computation.13 | async-start | bytes 6266880
  451.2 69.7 %copy-start.39 = (f32[288]{0:T(512)S(1)}, f32[288]{0:T(512)}, u32[]{:S(2)}) copy-start(f32[288]{0:T(512)} %param.45) | copy-start | bytes 3460
  451.2 133.4 %all-gather.12.cloned.1.call-start = ((), (), s32[]{:S(2)}) async-start(), calls=%async_computation.8 | async-start | bytes 6266880 | tf_op jit(solution)/shard_map/all_gather | solution.py:60
  520.9 16.3 %copy-start.2 = (bf16[2064,288]{1,0:T(8,128)(2,1)S(1)}, bf16[2064,288]{1,0:T(8,128)(2,1)}, u32[]{:S(2)}) copy-start(bf16[2064,288]{1,0:T(8,128)(2,1)} %copy.114) | copy-start | bytes 3566596
  542.2 42.5 %copy-start.45 = (bf16[288,1152]{1,0:T(8,128)(2,1)S(1)}, bf16[288,1152]{1,0:T(8,128)(2,1)}, u32[]{:S(2)}) copy-start(bf16[288,1152]{1,0:T(8,128)(2,1)} %param.38) | copy-start | bytes 1990660
  544.8 200.1 %reduce-scatter.24.cloned.1.call-start = ((), (), s32[]{:S(2)}) async-start(), calls=%async_computation.14 | async-start | bytes 6266880
  694.9 52.6 %copy-start.27 = (f32[2064]{0:T(1024)S(1)}, f32[2064]{0:T(1024)}, u32[]{:S(2)}) copy-start(f32[2064]{0:T(1024)} %copy-done.26) | copy-start | bytes 24772
  694.9 52.6 %copy-start.29 = (f32[2064]{0:T(1024)S(1)}, f32[2064]{0:T(1024)}, u32[]{:S(2)}) copy-start(f32[2064]{0:T(1024)} %copy-done.28) | copy-start | bytes 24772
  694.9 52.6 %copy-start.31 = (f32[288]{0:T(512)S(1)}, f32[288]{0:T(512)}, u32[]{:S(2)}) copy-start(f32[288]{0:T(512)} %param.34) | copy-start | bytes 3460
  694.9 52.6 %copy-start.34 = (f32[288]{0:T(512)S(1)}, f32[288]{0:T(512)}, u32[]{:S(2)}) copy-start(f32[288]{0:T(512)} %param.35) | copy-start | bytes 3460
  694.9 67.5 %copy-start.4 = (bf16[288,2064]{0,1:T(8,128)(2,1)S(1)}, bf16[288,2064]{0,1:T(8,128)(2,1)}, u32[]{:S(2)}) copy-start(bf16[288,2064]{0,1:T(8,128)(2,1)} %get-tuple-element.203) | copy-start | bytes 3566596
  694.9 115.0 %all-gather.14.cloned.1.call-start = ((), (), s32[]{:S(2)}) async-start(), calls=%async_computation.9 | async-start | bytes 6266880 | tf_op jit(solution)/shard_map/all_gather | solution.py:60
  770.1 343.8 %all-reduce.8.cloned.1.call-start = ((), (), s32[]{:S(2)}) async-start(), calls=%async_computation.15 | async-start | bytes 18579456 | tf_op jit(solution)/shard_map/psum | solution.py:264
  770.1 23.9 %slice-start.2 = ((s8[5013504]{0:T(1024)(128)(4,1)}), s8[4194304]{0:T(1024)(128)(4,1)S(1)}, s32[]{:S(2)}) async-start(s8[5013504]{0:T(1024)(128)(4,1)} %bitcast.211), calls=%async_computation.18 | async-start | bytes 8388608
  770.1 26.8 %slice-start = ((s8[5013504]{0:T(1024)(128)(4,1)}), s8[4194304]{0:T(1024)(128)(4,1)S(1)}, s32[]{:S(2)}) async-start(s8[5013504]{0:T(1024)(128)(4,1)} %bitcast.209), calls=%async_computation.16 | async-start | bytes 8388608
  781.6 15.3 %slice-start.1 = ((s8[5013504]{0:T(1024)(128)(4,1)}), s8[819200]{0:T(1024)(128)(4,1)S(1)}, s32[]{:S(2)}) async-start(s8[5013504]{0:T(1024)(128)(4,1)} %bitcast.209), calls=%async_computation.17 | async-start | bytes 1638400
  819.5 47.6 %copy-start.22 = (bf16[288,1152]{1,0:T(8,128)(2,1)S(1)}, bf16[288,1152]{1,0:T(8,128)(2,1)}, u32[]{:S(2)}) copy-start(bf16[288,1152]{1,0:T(8,128)(2,1)} %param.32) | copy-start | bytes 1990660
  (34 other events, 156.8 us)
Sparse Core Ops, SparseCore 0:
  19.0 84.3 reduce-scatter.15
  126.5 39.6 all-gather.5
  250.5 49.8 reduce-scatter.17
  324.2 39.6 all-gather.7
  365.9 39.0 all-gather.9
  415.4 49.8 reduce-scatter.19
  468.4 49.8 reduce-scatter.21
  545.0 39.6 all-gather.11
  695.0 49.8 reduce-scatter.23
  770.2 39.7 all-gather.13
  818.3 295.5 all-reduce.7
where the time goes:
time: 1140 us
  waiting for transfers between devices  601 us (53%)
  matrix products  221 us (19%)
  local copies, waits for them, and re-layouts  152 us (13%)
  blocking collectives  80.5 us (7%)
  other arithmetic  64.8 us (6%)
  between operations  15.4 us (1%)
    unnamed x16, waiting for transfers between devices  249 us
    psum x1, waiting for transfers between devices, body(): lax.psum(g_w_main.astype(jnp.bfloat16), 'dp').astype(jnp.float32)  236 us
    all_gather x2, waiting for transfers between devices, layer_norm(): return (normed, rstd, lax.all_gather(rounded, 'tp', axis=0, tiled=True))  69.8 us
    unnamed x123, local copies, waits for them, and re-layouts  63.8 us
    all_gather x3, waiting for transfers between devices, fold_back(): piece = lax.all_gather(shard, 'tp', axis=0, tiled=True)  46 us
    psum x1, blocking collectives, body(): lax.psum(g_b_skip.astype(jnp.bfloat16), 'dp').astype(jnp.float32)  39.2 us
    dot_general x4, matrix products, fold_back(): jnp.einsum('fc,ct->ft', weight, piece, preferred_element_type=jnp.float32)  32.7 us
    dot_general x1, matrix products, body(): jnp.einsum('dc,dt->ct', w_up, full_two, preferred_element_type=jnp.float32)  32.2 us
  transfers between devices with their start and end apart: 11, of which 10 were waited for; matrix products, arithmetic and copies ran while one was open for 13% of the time, Pallas kernels for 0%

commit v1 on v0

--- a/solution.py
+++ b/solution.py
@@ -126,7 +126,7 @@
     return (d_query.astype(jnp.bfloat16), d_key.astype(jnp.bfloat16), d_value.astype(jnp.bfloat16))
 
 
-def body(
+def body_features(
     main,
     long_skip,
     cotangent,
@@ -299,9 +299,412 @@
     )
 
 
+ITEM_ROWS = 264
+CORE = ("tp", 1)
+ACROSS_Y = ("tp", 2)
+ACROSS_X = ("dp", 1)
+ACROSS_Z = ("dp", 2)
+FAR_Z = ("dp", 4)
+
+
+def swap(value, link):
+    axis, bit = link
+    return lax.ppermute(value, axis, [(i, i ^ bit) for i in range(lax.axis_size(axis))])
+
+
+def side(link):
+    axis, bit = link
+    return (lax.axis_index(axis) // bit) % 2
+
+
+def in_order(bit, mine, theirs):
+    flip = bit == 1
+    return jnp.stack([jnp.where(flip, theirs, mine), jnp.where(flip, mine, theirs)])
+
+
+def pick(value, index):
+    return lax.dynamic_index_in_dim(value, index, 0, keepdims=False)
+
+
+def gather_peer_shard(shard, first, second):
+    rows, cols = shard.shape
+    quarters = shard.reshape(2, 2, rows // 4, cols)
+    mine = pick(pick(quarters, side(second)), side(first))
+    got = swap(mine, ACROSS_Y)
+    pair = in_order(side(first), got, swap(got, first))
+    whole = in_order(side(second), pair, swap(pair, second))
+    return whole.reshape(rows, cols)
+
+
+def add_low(mine, theirs):
+    return (mine.astype(jnp.float32) + theirs.astype(jnp.float32)).astype(jnp.bfloat16)
+
+
+def reduce_shard(mine, other, first, second):
+    rows, cols = mine.shape
+    total = add_low(mine, swap(other, ACROSS_Y))
+    for link in (first, second):
+        bit = side(link)
+        halves = total.reshape(2, -1, cols)
+        total = add_low(pick(halves, bit), swap(pick(halves, 1 - bit), link))
+    total = add_low(total, swap(total, FAR_Z))
+    for link in (second, first):
+        total = in_order(side(link), total, swap(total, link)).reshape(-1, cols)
+    return total
+
+
+def spread_tokens(block):
+    cols = block.shape[1]
+    padded = jnp.pad(block.reshape(-1, SEQ, cols), ((0, 0), (0, ITEM_ROWS - SEQ), (0, 0)))
+    return padded.reshape(2, 2, -1, cols)
+
+
+def exchange_in(block):
+    tokens = spread_tokens(block)
+    y, core = side(ACROSS_Y), side(CORE)
+    near = pick(tokens, y)
+    far = swap(pick(tokens, 1 - y), ACROSS_Y)
+    both = jnp.concatenate([near, far], axis=2)
+    mine = pick(both, core)
+    theirs = pick(both, 1 - core)
+    return mine, theirs, swap(theirs, CORE)
+
+
+def exchange_out(own_half, partner_half):
+    core, y = side(CORE), side(ACROSS_Y)
+    both = in_order(core, own_half, swap(partner_half, CORE))
+    width = own_half.shape[1] // 2
+    near, far = both[:, :, :width], both[:, :, width:]
+    tokens = in_order(y, near, swap(far, ACROSS_Y))
+    return tokens.reshape(-1, ITEM_ROWS, width)[:, :SEQ].reshape(-1, width)
+
+
+def natural(own_half, partner_half, width, axis):
+    flip_y, flip_core = side(ACROSS_Y) == 1, side(CORE) == 1
+    r0, r2 = jnp.split(own_half, 2, axis)
+    r1, r3 = jnp.split(partner_half, 2, axis)
+    a0, a2 = jnp.where(flip_y, r2, r0), jnp.where(flip_y, r0, r2)
+    a1, a3 = jnp.where(flip_y, r3, r1), jnp.where(flip_y, r1, r3)
+    b0, b1 = jnp.where(flip_core, a1, a0), jnp.where(flip_core, a0, a1)
+    b2, b3 = jnp.where(flip_core, a3, a2), jnp.where(flip_core, a2, a3)
+    return (b0, b1, b2, b3)
+
+
+def by_distance(blocks):
+    flip_y, flip_core = side(ACROSS_Y) == 1, side(CORE) == 1
+    b0, b1, b2, b3 = blocks
+    a0, a1 = jnp.where(flip_core, b1, b0), jnp.where(flip_core, b0, b1)
+    a2, a3 = jnp.where(flip_core, b3, b2), jnp.where(flip_core, b2, b3)
+    r0, r2 = jnp.where(flip_y, a2, a0), jnp.where(flip_y, a0, a2)
+    r1, r3 = jnp.where(flip_y, a3, a1), jnp.where(flip_y, a1, a3)
+    return r0, r1, r2, r3
+
+
+def dot(spec, left, right):
+    return jnp.einsum(spec, left, right, preferred_element_type=jnp.float32)
+
+
+def low(value):
+    return value.astype(jnp.bfloat16)
+
+
+def norm_rows(stream, gain, bias):
+    mean = jnp.mean(stream, 1, keepdims=True)
+    square = jnp.mean(stream * stream, 1, keepdims=True)
+    rstd = lax.rsqrt(square - mean * mean + EPSILON)
+    normed = (stream - mean) * rstd
+    return normed, rstd, low(normed * gain + bias)
+
+
+def norm_rows_back(d_out, normed, rstd, gain):
+    g_gain = jnp.sum(d_out * normed, 0)
+    g_bias = jnp.sum(d_out, 0)
+    scaled = d_out * gain
+    first = jnp.mean(scaled, 1, keepdims=True)
+    second = jnp.mean(scaled * normed, 1, keepdims=True)
+    return rstd * (scaled - first - normed * second), g_gain, g_bias
+
+
+def heads_of(rows):
+    return rows.reshape(-1, ITEM_ROWS, rows.shape[1] // HEAD, HEAD)
+
+
+def item_scores(query, key):
+    scores = dot("bqhd,bkhd->bhqk", query, key) * (1.0 / math.sqrt(HEAD))
+    present = lax.broadcasted_iota(jnp.int32, scores.shape, 3) < SEQ
+    return jnp.where(present, scores, -1e30)
+
+
+def item_attend(query, key, value):
+    query, key, value = heads_of(query), heads_of(key), heads_of(value)
+    scores = item_scores(query, key)
+    peak = jnp.max(scores, axis=-1, keepdims=True)
+    logsum = peak + jnp.log(jnp.sum(jnp.exp(scores - peak), axis=-1, keepdims=True))
+    probs = low(jnp.exp(scores - logsum))
+    out = low(dot("bhqk,bkhd->bqhd", probs, value))
+    return out.reshape(-1, out.shape[2] * HEAD), logsum
+
+
+def item_attend_back(query, key, value, logsum, d_out):
+    query, key, value, d_out = heads_of(query), heads_of(key), heads_of(value), heads_of(d_out)
+    scale = 1.0 / math.sqrt(HEAD)
+    probs = jnp.exp(item_scores(query, key) - logsum)
+    d_probs = dot("bqhd,bkhd->bhqk", d_out, value)
+    delta = jnp.sum(probs * d_probs, axis=-1, keepdims=True)
+    d_scores = low(probs * (d_probs - delta))
+    d_query = low(dot("bhqk,bkhd->bqhd", d_scores, key) * scale)
+    d_key = low(dot("bhqk,bqhd->bkhd", d_scores, query) * scale)
+    d_value = low(dot("bhqk,bqhd->bkhd", low(probs), d_out))
+    flat = lambda a: a.reshape(-1, a.shape[2] * HEAD)
+    return flat(d_query), flat(d_key), flat(d_value)
+
+
+def body_items(
+    main,
+    long_skip,
+    cotangent,
+    timesteps,
+    loss_codes,
+    code_weights,
+    item_counts,
+    w_skip_main,
+    w_skip_long,
+    b_skip,
+    ln1_gain,
+    ln1_bias,
+    w_qkv,
+    w_proj,
+    b_proj,
+    ln2_gain,
+    ln2_bias,
+    w_up,
+    b_up,
+    w_down,
+    b_down,
+):
+    local = main.shape[1]
+    width = 4 * local
+    rank = lax.axis_index("tp")
+    a_order, b_order = (ACROSS_X, ACROSS_Z), (ACROSS_Z, ACROSS_X)
+
+    vectors = jnp.concatenate(
+        [jnp.stack([b_skip, ln1_gain, ln1_bias, b_proj, ln2_gain, ln2_bias, b_down]), b_up.reshape(4, local)]
+    )
+    own_vectors = jnp.concatenate([vectors, swap(vectors, ACROSS_Y)], axis=1)
+    partner_vectors = swap(own_vectors, CORE)
+    joined = jnp.concatenate(natural(own_vectors[:7], partner_vectors[:7], local, 1), axis=1)
+    b_skip_all, gain_one, bias_one, b_proj_all, gain_two, bias_two, b_down_all = (
+        joined[k : k + 1] for k in range(7)
+    )
+
+    def up_vector(pair):
+        near, far = jnp.split(pair[7:], 2, 1)
+        return jnp.concatenate([near.reshape(1, -1), far.reshape(1, -1)], axis=1)
+
+    b_up_own, b_up_partner = up_vector(own_vectors), up_vector(partner_vectors)
+
+    main_own, main_pass, main_partner = exchange_in(main)
+    long_own, long_pass, long_partner = exchange_in(long_skip)
+
+    def halves(shard, order):
+        own = jnp.stack([shard, gather_peer_shard(shard, *order)])
+        return own, swap(own, CORE)
+
+    wm_own, wm_partner = halves(w_skip_main, a_order)
+    wl_own, wl_partner = halves(w_skip_long, b_order)
+    qkv_rows = jnp.swapaxes(w_qkv, 1, 2)
+    wq = halves(qkv_rows[0], a_order)
+    wk = halves(qkv_rows[1], b_order)
+    wv = halves(qkv_rows[2], a_order)
+    wp_own, wp_partner = halves(w_proj, b_order)
+
+    def tall(shard):
+        top = gather_peer_shard(shard[: 2 * local], *a_order)
+        bottom = gather_peer_shard(shard[2 * local :], *b_order)
+        own = jnp.stack([shard, jnp.concatenate([top, bottom])])
+        return own, swap(own, CORE)
+
+    wu_own, wu_partner = tall(w_up)
+    wd_own, wd_partner = tall(w_down)
+    cot_own, cot_pass, cot_partner = exchange_in(cotangent)
+
+    flat = lambda w: w.reshape(-1, w.shape[-1])
+    stream = (
+        dot("td,dc->tc", main_own, flat(wm_own))
+        + dot("td,dc->tc", main_partner, flat(wm_partner))
+        + dot("td,dc->tc", long_own, flat(wl_own))
+        + dot("td,dc->tc", long_partner, flat(wl_partner))
+        + b_skip_all
+    )
+    normed_one, rstd_one, full_one = norm_rows(stream, gain_one, bias_one)
+    n1_other = swap(full_one, CORE)
+    projected = jnp.zeros_like(stream)
+    kept = []
+    for side_at in (0, 1):
+        query, key, value = (low(dot("td,cd->tc", full_one, flat(w[side_at]))) for w in (wq, wk, wv))
+        attended, logsum = item_attend(query, key, value)
+        kept.append((query, key, value, logsum, attended))
+        projected = projected + dot("tc,cd->td", attended, flat((wp_own, wp_partner)[side_at]))
+    attended_other = swap(kept[1][4], CORE)
+    stream_two = stream + projected + b_proj_all
+    normed_two, rstd_two, full_two = norm_rows(stream_two, gain_two, bias_two)
+    n2_other = swap(full_two, CORE)
+
+    def up(weight, bias):
+        near = dot("td,dc->tc", full_two, weight[0])
+        far = dot("td,dc->tc", full_two, weight[1])
+        return jnp.concatenate([near, far], axis=1) + bias
+
+    up_own, up_partner = up(wu_own, b_up_own), up(wu_partner, b_up_partner)
+    act_own, act_partner = (low(jax.nn.gelu(u, approximate=False)) for u in (up_own, up_partner))
+    act_other = swap(act_partner, CORE)
+
+    item_scale, valid = item_factors(timesteps, loss_codes, code_weights, item_counts[0])
+    my_scale = pick(item_scale.reshape(4, -1), rank)
+    my_valid = pick(valid.reshape(4, -1), rank)
+    row_scale = jnp.repeat(my_scale, ITEM_ROWS)[:, None]
+    row_valid = jnp.repeat(my_valid, ITEM_ROWS)[:, None]
+    cot_rows = jnp.concatenate(natural(cot_own, cot_partner, local, 1), axis=1)
+    grad_low = low(cot_rows.astype(jnp.float32) * row_scale)
+    grad_other = swap(grad_low, CORE)
+    grad_wide = grad_low.astype(jnp.float32)
+    g_b_down = jnp.sum(grad_wide, 0)
+
+    both = lambda mine, other: jnp.concatenate([mine, other], axis=0)
+    grad_both = both(grad_low, grad_other)
+
+    def weight_grad(left, right):
+        return low(dot("tf,tc->fc", left, right))
+
+    down_part = weight_grad(both(act_own, act_other), grad_both).reshape(2, -1, width)
+
+    def reduce_tall(part):
+        cut = 2 * local
+        return jnp.concatenate(
+            [
+                reduce_shard(part[0, :cut], part[1, :cut], *a_order),
+                reduce_shard(part[0, cut:], part[1, cut:], *b_order),
+            ]
+        )
+
+    g_w_down = reduce_tall(down_part)
+
+    result = (
+        stream_two
+        + dot("tf,fc->tc", act_own, flat(wd_own))
+        + dot("tf,fc->tc", act_partner, flat(wd_partner))
+        + b_down_all
+    )
+    out_rows = low(result * row_valid)
+    pieces = by_distance(jnp.split(out_rows, 4, 1))
+    out = exchange_out(
+        jnp.concatenate([pieces[0], pieces[2]], axis=1), jnp.concatenate([pieces[1], pieces[3]], axis=1)
+    )
+
+    def up_back(upward, weight):
+        d_act = dot("tc,fc->tf", grad_low, flat(weight))
+        cumulative = 0.5 * (1.0 + lax.erf(upward * ROOT_HALF))
+        density = jnp.exp(-0.5 * upward * upward) * DENSITY_SCALE
+        return low(d_act * (cumulative + upward * density))
+
+    d_up_partner = up_back(up_partner, wd_partner)
+    d_up_other = swap(d_up_partner, CORE)
+    d_up_own = up_back(up_own, wd_own)
+    g_b_up_own = jnp.sum(d_up_own.astype(jnp.float32), 0)
+    g_b_up_partner = jnp.sum(d_up_partner.astype(jnp.float32), 0)
+    d_up_both = both(d_up_own, d_up_other)
+    n2_both = both(full_two, n2_other)
+    cut = d_up_own.shape[1] // 2
+    up_part = jnp.stack(
+        [weight_grad(n2_both, d_up_both[:, :cut]), weight_grad(n2_both, d_up_both[:, cut:])]
+    )
+    g_w_up = reduce_tall(up_part)
+
+    def up_term(d_up, weight):
+        return dot("tf,cf->tc", d_up[:, :cut], weight[0]) + dot("tf,cf->tc", d_up[:, cut:], weight[1])
+
+    d_n2 = up_term(d_up_own, wu_own) + up_term(d_up_partner, wu_partner)
+    back_two, g_ln2_gain, g_ln2_bias = norm_rows_back(d_n2, normed_two, rstd_two, gain_two)
+    d_stream_two = low(back_two + grad_wide)
+    d_stream_two_other = swap(d_stream_two, CORE)
+    d_stream_wide = d_stream_two.astype(jnp.float32)
+    g_b_proj = jnp.sum(d_stream_wide, 0)
+    proj_part = weight_grad(
+        both(kept[0][4], attended_other), both(d_stream_two, d_stream_two_other)
+    ).reshape(2, -1, width)
+    g_w_proj = reduce_shard(proj_part[0], proj_part[1], *b_order)
+
+    d_qkv = []
+    for side_at in (1, 0):
+        d_attended = low(dot("tc,fc->tf", d_stream_two, flat((wp_own, wp_partner)[side_at])))
+        d_qkv.append(item_attend_back(*kept[side_at][:4], d_attended))
+    d_partner, d_own = d_qkv
+    n1_both = both(full_one, n1_other)
+    g_w_qkv = []
+    d_n1 = jnp.zeros_like(d_n2)
+    for k, (w, order) in enumerate(((wq, a_order), (wk, a_order), (wv, a_order))):
+        part = weight_grad(both(d_own[k], swap(d_partner[k], CORE)), n1_both).reshape(2, -1, width)
+        g_w_qkv.append(reduce_shard(part[0], part[1], *order))
+        d_n1 = d_n1 + dot("tc,cd->td", d_own[k], flat(w[0])) + dot("tc,cd->td", d_partner[k], flat(w[1]))
+    back_one, g_ln1_gain, g_ln1_bias = norm_rows_back(d_n1, normed_one, rstd_one, gain_one)
+    d_stream = low(back_one + d_stream_wide)
+    d_stream_both = both(d_stream, swap(d_stream, CORE))
+    g_b_skip = jnp.sum(d_stream.astype(jnp.float32), 0)
+
+    core = side(CORE)
+
+    def skip_parts(own, passed, other_rows, order):
+        part = weight_grad(both(own, other_rows), d_stream_both).reshape(2, -1, width)
+        return reduce_shard(part[0], part[1], *order)
+
+    g_w_main = skip_parts(main_own, None, main_pass, a_order)
+    g_w_long = skip_parts(long_own, None, long_pass, b_order)
+    d_main = exchange_out(
+        low(dot("tc,fc->tf", d_stream, flat(wm_own))), low(dot("tc,fc->tf", d_stream, flat(wm_partner)))
+    )
+    d_long = exchange_out(
+        low(dot("tc,fc->tf", d_stream, flat(wl_own))), low(dot("tc,fc->tf", d_stream, flat(wl_partner)))
+    )
+
+    b_up_blocks = natural(
+        g_b_up_own.reshape(2, -1), g_b_up_partner.reshape(2, -1), 0, 0
+    )
+    small = jnp.concatenate(
+        [
+            jnp.stack([g_b_skip, g_ln1_gain, g_ln1_bias, g_b_proj, g_ln2_gain, g_ln2_bias, g_b_down]),
+            jnp.concatenate(b_up_blocks, axis=0),
+        ]
+    )
+    for link in (CORE, ACROSS_X, ACROSS_Z, ACROSS_Y, FAR_Z):
+        small = small + swap(small, link)
+    mine = pick(jnp.stack(jnp.split(small[:7], 4, 1)), rank)
+    g_b_up = pick(small[7:], rank)
+    wide = lambda a: a.astype(jnp.float32)
+    return (
+        out,
+        d_main,
+        d_long,
+        wide(g_w_main),
+        wide(g_w_long),
+        mine[0],
+        mine[1],
+        mine[2],
+        jnp.stack([wide(g.T) for g in g_w_qkv]),
+        wide(g_w_proj),
+        mine[3],
+        mine[4],
+        mine[5],
+        wide(g_w_up),
+        g_b_up,
+        wide(g_w_down),
+        mine[6],
+    )
+
+
 def solution(mesh):
+    by_items = mesh.shape["tp"] == 4 and mesh.shape["dp"] == 8
     return jax.shard_map(
-        body,
+        body_items if by_items else body_features,
         mesh=mesh,
         in_specs=(
             P("dp", "tp"),

time: 1140 us -> 1120 us (0.982)
  waiting for transfers between devices: 601 us -> 438 us
  starting transfers between devices: 0.67 us -> 119 us
  blocking collectives: 80.5 us -> 0 us
  other arithmetic: 64.8 us -> 122 us
  local copies, waits for them, and re-layouts: 152 us -> 188 us
  matrix products: 221 us -> 236 us
    ppermute x0 -> x128, waiting for transfers between devices: none -> 438 us  [swap(): lax.ppermute(value, axis, [(i, i ^ bit) for i in range(lax.axis_size(axis...]
    unnamed x16 -> x0, waiting for transfers between devices: 249 us -> none
    psum x1 -> x0, waiting for transfers between devices: 236 us -> none  [body(): lax.psum(g_w_main.astype(jnp.bfloat16), 'dp').astype(jnp.float32)]
    ppermute x0 -> x128, starting transfers between devices: none -> 119 us  [swap(): lax.ppermute(value, axis, [(i, i ^ bit) for i in range(lax.axis_size(axis...]
    all_gather x5 -> x0, waiting for transfers between devices: 116 us -> none  [the longest x2 69.8 us: layer_norm(): return (normed, rstd, lax.all_gather(rounded, 'tp', axis=0, tiled=True))]
    psum x5 -> x0, blocking collectives: 80.5 us -> none  [the longest x1 39.2 us: body(): lax.psum(g_b_skip.astype(jnp.bfloat16), 'dp').astype(jnp.float32)]
    reshape x3 -> x43, local copies, waits for them, and re-layouts: 12.7 us -> 80.6 us  [the longest x16 36.6 us: heads_of(): return rows.reshape(-1, ITEM_ROWS, rows.shape[1] // HEAD, HEAD)]
    another operation x0 -> x103, other arithmetic: none -> 50.1 us  [the longest x91 34.3 us: in_order(): jnp.stack([jnp.where(flip, theirs, mine), jnp.where(flip, mine, theirs)])]
  transfers between devices with their start and end apart: 11 -> 128, of which waited for: 10 -> 63; matrix products, arithmetic and copies ran while one was open for 13% -> 47% of each run, Pallas kernels for 0% -> 0%
where the time goes in v1:
time: 1120 us; the launch traced here: 1110 us
  waiting for transfers between devices  438 us (39%)
  matrix products  236 us (21%)
  local copies, waits for them, and re-layouts  188 us (17%)
  other arithmetic  122 us (11%)
  starting transfers between devices  119 us (11%)
    ppermute x128, waiting for transfers between devices, swap(): lax.ppermute(value, axis, [(i, i ^ bit) for i in range(lax.axis_size(axis...  438 us
    dot_general x57, matrix products, dot(): return jnp.einsum(spec, left, right, preferred_element_type=jnp.float32)  236 us
    ppermute x128, starting transfers between devices, swap(): lax.ppermute(value, axis, [(i, i ^ bit) for i in range(lax.axis_size(axis...  119 us
    reshape x16, local copies, waits for them, and re-layouts, heads_of(): return rows.reshape(-1, ITEM_ROWS, rows.shape[1] // HEAD, HEAD)  36.6 us
    another operation x91, other arithmetic, in_order(): jnp.stack([jnp.where(flip, theirs, mine), jnp.where(flip, mine, theirs)])  34.3 us
    convert_element_type x5, other arithmetic, low(): return value.astype(jnp.bfloat16)  34 us
  transfers between devices with their start and end apart: 128, of which 63 were waited for; matrix products, arithmetic and copies ran while one was open for 47% of the time, Pallas kernels for 0%

profile of v1, /device:TPU:0, one launch (start us, length us, event | category | flops | bytes accessed | tf_op | source)
XLA Modules:
  0.0 1107.8 jit_solution(16280356419691032004)
XLA Ops:
  65.7 11.9 %collective-permute-done.20 = bf16[72,1152]{1,0:T(8,128)(2,1)S(1)} collective-permute-done((bf16[72,1152]{1,0:T(8,128)(2,1)}, bf16[72,1152]{1,0:T(8,128)(2,1)S(1)}, u32[]{:S(2)}, u32[]{:S(2)}) %collective-permute-start.20) | collective-permute-done | bytes 165920 | tf_op jit(solution)/shard_map/ppermute | solution.py:312
  86.0 13.4 %collective-permute-done.17 = bf16[72,1152]{1,0:T(8,128)(2,1)S(1)} collective-permute-done((bf16[72,1152]{1,0:T(8,128)(2,1)}, bf16[72,1152]{1,0:T(8,128)(2,1)S(1)}, u32[]{:S(2)}, u32[]{:S(2)}) %collective-permute-start.17) | collective-permute-done | bytes 165920 | tf_op jit(solution)/shard_map/ppermute | solution.py:312
  136.0 7.4 collective-permute-done.9
  145.0 8.6 collective-permute-done.25
  210.8 15.3 %collective-permute-done.38 = bf16[2,144,1152]{2,1,0:T(8,128)(2,1)S(1)} collective-permute-done((bf16[2,144,1152]{2,1,0:T(8,128)(2,1)S(1)}, bf16[2,144,1152]{2,1,0:T(8,128)(2,1)S(1)}, u32[]{:S(2)}, u32[]{:S(2)}) %collective-permute-start.38) | collective-permute-done | bytes 663584 | tf_op jit(solution)/shard_map/ppermute | solution.py:312
  227.2 15.2 %collective-permute-done.35 = bf16[2,144,1152]{2,1,0:T(8,128)(2,1)S(1)} collective-permute-done((bf16[2,144,1152]{2,1,0:T(8,128)(2,1)S(1)}, bf16[2,144,1152]{2,1,0:T(8,128)(2,1)S(1)}, u32[]{:S(2)}, u32[]{:S(2)}) %collective-permute-start.35) | collective-permute-done | bytes 663584 | tf_op jit(solution)/shard_map/ppermute | solution.py:312
  246.1 11.7 %collective-permute-done.32 = bf16[2,144,1152]{2,1,0:T(8,128)(2,1)S(1)} collective-permute-done((bf16[2,144,1152]{2,1,0:T(8,128)(2,1)S(1)}, bf16[2,144,1152]{2,1,0:T(8,128)(2,1)S(1)}, u32[]{:S(2)}, u32[]{:S(2)}) %collective-permute-start.32) | collective-permute-done | bytes 663584 | tf_op jit(solution)/shard_map/ppermute | solution.py:312
  382.7 11.5 %fusion.6 = bf16[528,2304]{1,0:T(8,128)(2,1)} fusion(f32[528,1152]{1,0:T(8,128)S(1)} %fusion.101, f32[528,1152]{1,0:T(8,128)S(1)} %fusion.161, f32[2304]{0:T(1024)S(1)} %maximum_reduce_fusion), kind=kLoop, calls=%fused_computation.27 | loop fusion | flops 81506304 | bytes 7308288 | tf_op jit(solution)/shard_map/convert_element_type | solution.py:408
  408.9 11.3 %fusion.9 = bf16[528,2304]{1,0:T(8,128)(2,1)} fusion(f32[528,1152]{1,0:T(8,128)S(1)} %fusion.61, f32[528,1152]{1,0:T(8,128)S(1)} %fusion.59, f32[2304]{0:T(1024)S(1)} %maximum_reduce_fusion.1), kind=kLoop, calls=%fused_computation.30 | loop fusion | flops 81506304 | bytes 7308288 | tf_op jit(solution)/shard_map/convert_element_type | solution.py:408
  420.2 7.7 convert_reduce_fusion.1
  468.7 14.6 %multiply_reduce_fusion = (f32[2,8,264]{2,1,0:T(8,128)S(1)}, f32[2,8,264]{2,1,0:T(8,128)S(1)}, f32[2,8,264,264]{2,3,1,0:T(8,128)}) fusion(f32[2,8,264,264]{2,3,1,0:T(8,128)} %copy-done.1, f32[2,8,264]{2,1,0:T(8,128)S(1)} %log_add_fusion, pred[264]{0:T(512)(128)(4,1)S(1)} %iota_compare_fusion.1, f32[2,8,264,264]{2,3,1,0:T(8,128)} %fusion.163, ...), kind=kOutput, calls=%fused_computation.10 | convolution fusion | flops 171722496 | bytes 19126536 | tf_op jit(solution)/shard_map/bqhd,bkhd->bhqk/dot_general | solution.py:404
  483.4 7.9 multiply_convert_fusion
  554.0 7.3 fusion.162
  572.9 7.3 multiply_convert_fusion.3
  663.1 14.3 %collective-permute-done.49 = bf16[2,528,288]{1,2,0:T(8,128)(2,1)} collective-permute-done((bf16[2,528,288]{1,2,0:T(8,128)(2,1)}, bf16[2,528,288]{1,2,0:T(8,128)(2,1)}, u32[]{:S(2)}, u32[]{:S(2)}) %collective-permute-start.49) | collective-permute-done | bytes 608288 | tf_op jit(solution)/shard_map/ppermute | solution.py:312
  694.3 11.5 %collective-permute-done.72 = bf16[288,1152]{1,0:T(8,128)(2,1)} collective-permute-done((bf16[288,1152]{1,0:T(8,128)(2,1)}, bf16[288,1152]{1,0:T(8,128)(2,1)}, u32[]{:S(2)}, u32[]{:S(2)}) %collective-permute-start.72) | collective-permute-done | bytes 663584 | tf_op jit(solution)/shard_map/ppermute | solution.py:312
  707.4 12.6 %collective-permute-done.79 = bf16[288,1152]{1,0:T(8,128)(2,1)S(1)} collective-permute-done((bf16[288,1152]{1,0:T(8,128)(2,1)}, bf16[288,1152]{1,0:T(8,128)(2,1)S(1)}, u32[]{:S(2)}, u32[]{:S(2)}) %collective-permute-start.79) | collective-permute-done | bytes 663584 | tf_op jit(solution)/shard_map/ppermute | solution.py:312
  721.8 6.9 collective-permute-done.87
  762.9 16.0 %collective-permute-done.59 = bf16[288,1152]{1,0:T(8,128)(2,1)S(1)} collective-permute-done((bf16[288,1152]{1,0:T(8,128)(2,1)S(1)}, bf16[288,1152]{1,0:T(8,128)(2,1)S(1)}, u32[]{:S(2)}, u32[]{:S(2)}) %collective-permute-start.59) | collective-permute-done | bytes 663584 | tf_op jit(solution)/shard_map/ppermute | solution.py:312
  780.2 15.1 %collective-permute-done.53 = bf16[288,1152]{1,0:T(8,128)(2,1)S(1)} collective-permute-done((bf16[288,1152]{1,0:T(8,128)(2,1)S(1)}, bf16[288,1152]{1,0:T(8,128)(2,1)S(1)}, u32[]{:S(2)}, u32[]{:S(2)}) %collective-permute-start.53) | collective-permute-done | bytes 663584 | tf_op jit(solution)/shard_map/ppermute | solution.py:312
  796.5 8.2 collective-permute-done.89
  804.8 9.5 collective-permute-done.75
  814.3 9.2 collective-permute-done.82
  841.1 8.7 collective-permute-done.95
  849.8 7.0 collective-permute-done.60
  896.0 9.9 convolution_convert_fusion
  945.8 9.1 collective-permute-done.64
  971.4 25.3 %collective-permute-done.116 = bf16[576,1152]{1,0:T(8,128)(2,1)S(1)} collective-permute-done((bf16[576,1152]{1,0:T(8,128)(2,1)S(1)}, bf16[576,1152]{1,0:T(8,128)(2,1)S(1)}, u32[]{:S(2)}, u32[]{:S(2)}) %collective-permute-start.116) | collective-permute-done | bytes 1327136 | tf_op jit(solution)/shard_map/ppermute | solution.py:312
  996.7 14.2 %collective-permute-done.122 = bf16[576,1152]{1,0:T(8,128)(2,1)S(1)} collective-permute-done((bf16[576,1152]{1,0:T(8,128)(2,1)S(1)}, bf16[576,1152]{1,0:T(8,128)(2,1)S(1)}, u32[]{:S(2)}, u32[]{:S(2)}) %collective-permute-start.122) | collective-permute-done | bytes 1327136 | tf_op jit(solution)/shard_map/ppermute | solution.py:312
  1024.5 9.7 collective-permute-done.123
  1036.3 9.6 collective-permute-done.104
  1057.8 6.9 collective-permute-done.111
  (961 shorter events, 747.9 us)
Async XLA Ops:
  6.4 40.4 %collective-permute-start.12 = (f32[11,288]{1,0:T(8,128)S(1)}, f32[11,288]{1,0:T(8,128)S(1)}, u32[]{:S(2)}, u32[]{:S(2)}) collective-permute-start(f32[11,288]{1,0:T(8,128)S(1)} %concatenate.98), channel_id=1, source_target_pairs={{0,2},{1,3},{2,0},{3,1},{4,6},{5,7},{6,4},{7,5},{8,10},{9,11},{10,... | collective-permute-start | bytes 38024 | tf_op jit(solution)/shard_map/ppermute | solution.py:312
  11.0 69.7 %collective-permute-start.1 = (bf16[72,1152]{1,0:T(8,128)(2,1)}, bf16[72,1152]{1,0:T(8,128)(2,1)}, u32[]{:S(2)}, u32[]{:S(2)}) collective-permute-start(bf16[72,1152]{1,0:T(8,128)(2,1)} %dynamic-slice_bitcast_fusion.31), channel_id=1, source_target_pairs={{0,2},{1,3},{2,0},{3,1},{4,6},{5,7},{6,4},{7,5},{8,10},{9,11},{10,... | collective-permute-start | bytes 497672 | tf_op jit(solution)/shard_map/ppermute | solution.py:312
  12.7 43.3 %collective-permute-start.7 = (bf16[72,1152]{1,0:T(8,128)(2,1)}, bf16[72,1152]{1,0:T(8,128)(2,1)}, u32[]{:S(2)}, u32[]{:S(2)}) collective-permute-start(bf16[72,1152]{1,0:T(8,128)(2,1)} %dynamic-slice_bitcast_fusion.30), channel_id=1, source_target_pairs={{0,2},{1,3},{2,0},{3,1},{4,6},{5,7},{6,4},{7,5},{8,10},{9,11},{10,... | collective-permute-start | bytes 497672 | tf_op jit(solution)/shard_map/ppermute | solution.py:312
  16.2 43.7 %collective-permute-start.23 = (bf16[72,1152]{1,0:T(8,128)(2,1)}, bf16[72,1152]{1,0:T(8,128)(2,1)}, u32[]{:S(2)}, u32[]{:S(2)}) collective-permute-start(bf16[72,1152]{1,0:T(8,128)(2,1)} %dynamic-slice_bitcast_fusion.26), channel_id=1, source_target_pairs={{0,2},{1,3},{2,0},{3,1},{4,6},{5,7},{6,4},{7,5},{8,10},{9,11},{10,... | collective-permute-start | bytes 497672 | tf_op jit(solution)/shard_map/ppermute | solution.py:312
  24.4 98.3 %collective-permute-start = (bf16[2,528,288]{1,2,0:T(8,128)(2,1)}, bf16[2,528,288]{1,2,0:T(8,128)(2,1)}, u32[]{:S(2)}, u32[]{:S(2)}) collective-permute-start(bf16[2,528,288]{1,2,0:T(8,128)(2,1)} %bitcast.2), channel_id=1, source_target_pairs={{0,2},{1,3},{2,0},{3,1},{4,6},{5,7},{6,4},{7,5},{8,10},{9,11},{10,... | collective-permute-start | bytes 1824776 | tf_op jit(solution)/shard_map/ppermute | solution.py:312
  55.0 70.6 %collective-permute-start.6 = (bf16[2,528,288]{1,2,0:T(8,128)(2,1)}, bf16[2,528,288]{1,2,0:T(8,128)(2,1)}, u32[]{:S(2)}, u32[]{:S(2)}) collective-permute-start(bf16[2,528,288]{1,2,0:T(8,128)(2,1)} %bitcast.742), channel_id=1, source_target_pairs={{0,2},{1,3},{2,0},{3,1},{4,6},{5,7},{6,4},{7,5},{8,10},{9,11},{10,... | collective-permute-start | bytes 1824776 | tf_op jit(solution)/shard_map/ppermute | solution.py:312
  104.8 59.0 %collective-permute-start.39 = (bf16[144,1152]{1,0:T(8,128)(2,1)}, bf16[144,1152]{1,0:T(8,128)(2,1)}, u32[]{:S(2)}, u32[]{:S(2)}) collective-permute-start(bf16[144,1152]{1,0:T(8,128)(2,1)} %dynamic-slice_bitcast_fusion.16), channel_id=1, source_target_pairs={{0,2},{1,3},{2,0},{3,1},{4,6},{5,7},{6,4},{7,5},{8,10},{9,11},{10,... | collective-permute-start | bytes 995336 | tf_op jit(solution)/shard_map/ppermute | solution.py:312
  110.7 55.1 %collective-permute-start.36 = (bf16[144,1152]{1,0:T(8,128)(2,1)}, bf16[144,1152]{1,0:T(8,128)(2,1)}, u32[]{:S(2)}, u32[]{:S(2)}) collective-permute-start(bf16[144,1152]{1,0:T(8,128)(2,1)} %dynamic-slice_bitcast_fusion.17), channel_id=1, source_target_pairs={{0,2},{1,3},{2,0},{3,1},{4,6},{5,7},{6,4},{7,5},{8,10},{9,11},{10,... | collective-permute-start | bytes 995336 | tf_op jit(solution)/shard_map/ppermute | solution.py:312
  122.7 43.2 %collective-permute-start.33 = (bf16[144,1152]{1,0:T(8,128)(2,1)}, bf16[144,1152]{1,0:T(8,128)(2,1)}, u32[]{:S(2)}, u32[]{:S(2)}) collective-permute-start(bf16[144,1152]{1,0:T(8,128)(2,1)} %dynamic-slice_bitcast_fusion.18), channel_id=1, source_target_pairs={{0,2},{1,3},{2,0},{3,1},{4,6},{5,7},{6,4},{7,5},{8,10},{9,11},{10,... | collective-permute-start | bytes 995336 | tf_op jit(solution)/shard_map/ppermute | solution.py:312
  125.5 41.8 %collective-permute-start.30 = (bf16[144,1152]{1,0:T(8,128)(2,1)}, bf16[144,1152]{1,0:T(8,128)(2,1)}, u32[]{:S(2)}, u32[]{:S(2)}) collective-permute-start(bf16[144,1152]{1,0:T(8,128)(2,1)} %dynamic-slice_bitcast_fusion.19), channel_id=1, source_target_pairs={{0,2},{1,3},{2,0},{3,1},{4,6},{5,7},{6,4},{7,5},{8,10},{9,11},{10,... | collective-permute-start | bytes 995336 | tf_op jit(solution)/shard_map/ppermute | solution.py:312
  177.2 86.3 %collective-permute-start.4 = (bf16[528,576]{1,0:T(8,128)(2,1)}, bf16[528,576]{1,0:T(8,128)(2,1)}, u32[]{:S(2)}, u32[]{:S(2)}) collective-permute-start(bf16[528,576]{1,0:T(8,128)(2,1)} %get-tuple-element.82), channel_id=1, source_target_pairs={{0,1},{1,0},{2,3},{3,2},{4,5},{5,4},{6,7},{7,6},{8,9},{9,8},{10,11... | collective-permute-start | bytes 1824776 | tf_op jit(solution)/shard_map/ppermute | solution.py:312
  180.7 88.7 %collective-permute-start.10 = (bf16[528,576]{1,0:T(8,128)(2,1)}, bf16[528,576]{1,0:T(8,128)(2,1)}, u32[]{:S(2)}, u32[]{:S(2)}) collective-permute-start(bf16[528,576]{1,0:T(8,128)(2,1)} %get-tuple-element.78), channel_id=1, source_target_pairs={{0,1},{1,0},{2,3},{3,2},{4,5},{5,4},{6,7},{7,6},{8,9},{9,8},{10,11... | collective-permute-start | bytes 1824776 | tf_op jit(solution)/shard_map/ppermute | solution.py:312
  187.5 76.5 %collective-permute-start.5 = (bf16[2,288,1152]{2,1,0:T(8,128)(2,1)}, bf16[2,288,1152]{2,1,0:T(8,128)(2,1)}, u32[]{:S(2)}, u32[]{:S(2)}) collective-permute-start(bf16[2,288,1152]{2,1,0:T(8,128)(2,1)} %pad_maximum_fusion.15), channel_id=1, source_target_pairs={{0,1},{1,0},{2,3},{3,2},{4,5},{5,4},{6,7},{7,6},{8,9},{9,8},{10,11... | collective-permute-start | bytes 3981320 | tf_op jit(solution)/shard_map/ppermute | solution.py:312
  199.5 70.4 %collective-permute-start.11 = (bf16[2,288,1152]{2,1,0:T(8,128)(2,1)}, bf16[2,288,1152]{2,1,0:T(8,128)(2,1)}, u32[]{:S(2)}, u32[]{:S(2)}) collective-permute-start(bf16[2,288,1152]{2,1,0:T(8,128)(2,1)} %pad_maximum_fusion.16), channel_id=1, source_target_pairs={{0,1},{1,0},{2,3},{3,2},{4,5},{5,4},{6,7},{7,6},{8,9},{9,8},{10,11... | collective-permute-start | bytes 3981320 | tf_op jit(solution)/shard_map/ppermute | solution.py:312
  257.9 104.9 %collective-permute-start.29 = (bf16[2,288,1152]{2,1,0:T(8,128)(2,1)}, bf16[2,288,1152]{2,1,0:T(8,128)(2,1)}, u32[]{:S(2)}, u32[]{:S(2)}) collective-permute-start(bf16[2,288,1152]{2,1,0:T(8,128)(2,1)} %pad_maximum_fusion.20), channel_id=1, source_target_pairs={{0,1},{1,0},{2,3},{3,2},{4,5},{5,4},{6,7},{7,6},{8,9},{9,8},{10,11... | collective-permute-start | bytes 3981320 | tf_op jit(solution)/shard_map/ppermute | solution.py:312
  263.4 68.4 %collective-permute-start.26 = (bf16[2,288,1152]{2,1,0:T(8,128)(2,1)}, bf16[2,288,1152]{2,1,0:T(8,128)(2,1)}, u32[]{:S(2)}, u32[]{:S(2)}) collective-permute-start(bf16[2,288,1152]{2,1,0:T(8,128)(2,1)} %pad_maximum_fusion.17), channel_id=1, source_target_pairs={{0,1},{1,0},{2,3},{3,2},{4,5},{5,4},{6,7},{7,6},{8,9},{9,8},{10,11... | collective-permute-start | bytes 3981320 | tf_op jit(solution)/shard_map/ppermute | solution.py:312
  269.9 623.1 %collective-permute-start.115 = (bf16[528,1152]{1,0:T(8,128)(2,1)}, bf16[528,1152]{1,0:T(8,128)(2,1)}, u32[]{:S(2)}, u32[]{:S(2)}) collective-permute-start(bf16[528,1152]{1,0:T(8,128)(2,1)} %get-tuple-element.50), channel_id=1, source_target_pairs={{0,1},{1,0},{2,3},{3,2},{4,5},{5,4},{6,7},{7,6},{8,9},{9,8},{10,11... | collective-permute-start | bytes 3649544 | tf_op jit(solution)/shard_map/ppermute | solution.py:312
  274.8 126.0 %collective-permute-start.42 = (bf16[2,1152,1152]{2,1,0:T(8,128)(2,1)}, bf16[2,1152,1152]{2,1,0:T(8,128)(2,1)}, u32[]{:S(2)}, u32[]{:S(2)}) collective-permute-start(bf16[2,1152,1152]{2,1,0:T(8,128)(2,1)} %pad_maximum_fusion.1), channel_id=1, source_target_pairs={{0,1},{1,0},{2,3},{3,2},{4,5},{5,4},{6,7},{7,6},{8,9},{9,8},{10,11... | collective-permute-start | bytes 15925256 | tf_op jit(solution)/shard_map/ppermute | solution.py:312
  282.3 137.9 %collective-permute-start.43 = (bf16[2,1152,1152]{2,1,0:T(8,128)(2,1)}, bf16[2,1152,1152]{2,1,0:T(8,128)(2,1)}, u32[]{:S(2)}, u32[]{:S(2)}) collective-permute-start(bf16[2,1152,1152]{2,1,0:T(8,128)(2,1)} %pad_maximum_fusion), channel_id=1, source_target_pairs={{0,1},{1,0},{2,3},{3,2},{4,5},{5,4},{6,7},{7,6},{8,9},{9,8},{10,11... | collective-permute-start | bytes 15925256 | tf_op jit(solution)/shard_map/ppermute | solution.py:312
  331.9 263.0 %collective-permute-start.71 = (bf16[528,1152]{1,0:T(8,128)(2,1)}, bf16[528,1152]{1,0:T(8,128)(2,1)}, u32[]{:S(2)}, u32[]{:S(2)}) collective-permute-start(bf16[528,1152]{1,0:T(8,128)(2,1)} %add_convert_fusion.1), channel_id=1, source_target_pairs={{0,1},{1,0},{2,3},{3,2},{4,5},{5,4},{6,7},{7,6},{8,9},{9,8},{10,11... | collective-permute-start | bytes 3649544 | tf_op jit(solution)/shard_map/ppermute | solution.py:312
  622.2 262.5 %collective-permute-start.100 = (bf16[528,1152]{1,0:T(8,128)(2,1)}, bf16[528,1152]{1,0:T(8,128)(2,1)}, u32[]{:S(2)}, u32[]{:S(2)}) collective-permute-start(bf16[528,1152]{1,0:T(8,128)(2,1)} %add_convert_fusion), channel_id=1, source_target_pairs={{0,1},{1,0},{2,3},{3,2},{4,5},{5,4},{6,7},{7,6},{8,9},{9,8},{10,11... | collective-permute-start | bytes 3649544 | tf_op jit(solution)/shard_map/ppermute | solution.py:312
  638.0 39.5 %collective-permute-start.49 = (bf16[2,528,288]{1,2,0:T(8,128)(2,1)}, bf16[2,528,288]{1,2,0:T(8,128)(2,1)}, u32[]{:S(2)}, u32[]{:S(2)}) collective-permute-start(bf16[2,528,288]{1,2,0:T(8,128)(2,1)} %copy.306), channel_id=1, source_target_pairs={{0,2},{1,3},{2,0},{3,1},{4,6},{5,7},{6,4},{7,5},{8,10},{9,11},{10,... | collective-permute-start | bytes 1824776 | tf_op jit(solution)/shard_map/ppermute | solution.py:312
  648.4 43.3 %collective-permute-start.86 = (bf16[288,1152]{1,0:T(8,128)(2,1)}, bf16[288,1152]{1,0:T(8,128)(2,1)}, u32[]{:S(2)}, u32[]{:S(2)}) collective-permute-start(bf16[288,1152]{1,0:T(8,128)(2,1)} %slice.320), channel_id=1, source_target_pairs={{0,2},{1,3},{2,0},{3,1},{4,6},{5,7},{6,4},{7,5},{8,10},{9,11},{10,... | collective-permute-start | bytes 1990664 | tf_op jit(solution)/shard_map/ppermute | solution.py:312
  661.6 223.6 %collective-permute-start.101 = (bf16[528,2304]{1,0:T(8,128)(2,1)}, bf16[528,2304]{1,0:T(8,128)(2,1)}, u32[]{:S(2)}, u32[]{:S(2)}) collective-permute-start(bf16[528,2304]{1,0:T(8,128)(2,1)} %copy-done.156), channel_id=1, source_target_pairs={{0,1},{1,0},{2,3},{3,2},{4,5},{5,4},{6,7},{7,6},{8,9},{9,8},{10,11... | collective-permute-start | bytes 7299080 | tf_op jit(solution)/shard_map/ppermute | solution.py:312
  705.9 55.6 %collective-permute-start.94 = (bf16[288,1152]{1,0:T(8,128)(2,1)}, bf16[288,1152]{1,0:T(8,128)(2,1)S(1)}, u32[]{:S(2)}, u32[]{:S(2)}) collective-permute-start(bf16[288,1152]{1,0:T(8,128)(2,1)} %slice.322), channel_id=1, source_target_pairs={{0,2},{1,3},{2,0},{3,1},{4,6},{5,7},{6,4},{7,5},{8,10},{9,11},{10,... | collective-permute-start | bytes 1990664 | tf_op jit(solution)/shard_map/ppermute | solution.py:312
  761.4 133.4 %collective-permute-start.114 = (bf16[528,2304]{1,0:T(8,128)(2,1)S(1)}, bf16[528,2304]{1,0:T(8,128)(2,1)S(1)}, u32[]{:S(2)}, u32[]{:S(2)}) collective-permute-start(bf16[528,2304]{1,0:T(8,128)(2,1)S(1)} %copy-done.72), channel_id=1, source_target_pairs={{0,1},{1,0},{2,3},{3,2},{4,5},{5,4},{6,7},{7,6},{8,9},{9,8},{10,11... | collective-permute-start | bytes 7299080 | tf_op jit(solution)/shard_map/ppermute | solution.py:312
  908.0 57.2 %collective-permute-start.102 = (bf16[576,1152]{1,0:T(8,128)(2,1)S(1)}, bf16[576,1152]{1,0:T(8,128)(2,1)S(1)}, u32[]{:S(2)}, u32[]{:S(2)}) collective-permute-start(bf16[576,1152]{1,0:T(8,128)(2,1)S(1)} %get-tuple-element.61), channel_id=1, source_target_pairs={{0,2},{1,3},{2,0},{3,1},{4,6},{5,7},{6,4},{7,5},{8,10},{9,11},{10,... | collective-permute-start | bytes 3981320 | tf_op jit(solution)/shard_map/ppermute | solution.py:312
  908.3 60.2 %collective-permute-start.108 = (bf16[576,1152]{1,0:T(8,128)(2,1)S(1)}, bf16[576,1152]{1,0:T(8,128)(2,1)S(1)}, u32[]{:S(2)}, u32[]{:S(2)}) collective-permute-start(bf16[576,1152]{1,0:T(8,128)(2,1)S(1)} %get-tuple-element.62), channel_id=1, source_target_pairs={{0,2},{1,3},{2,0},{3,1},{4,6},{5,7},{6,4},{7,5},{8,10},{9,11},{10,... | collective-permute-start | bytes 3981320 | tf_op jit(solution)/shard_map/ppermute | solution.py:312
  918.8 77.9 %collective-permute-start.116 = (bf16[576,1152]{1,0:T(8,128)(2,1)S(1)}, bf16[576,1152]{1,0:T(8,128)(2,1)S(1)}, u32[]{:S(2)}, u32[]{:S(2)}) collective-permute-start(bf16[576,1152]{1,0:T(8,128)(2,1)S(1)} %get-tuple-element.57), channel_id=1, source_target_pairs={{0,2},{1,3},{2,0},{3,1},{4,6},{5,7},{6,4},{7,5},{8,10},{9,11},{10,... | collective-permute-start | bytes 3981320 | tf_op jit(solution)/shard_map/ppermute | solution.py:312
  918.9 92.0 %collective-permute-start.122 = (bf16[576,1152]{1,0:T(8,128)(2,1)S(1)}, bf16[576,1152]{1,0:T(8,128)(2,1)S(1)}, u32[]{:S(2)}, u32[]{:S(2)}) collective-permute-start(bf16[576,1152]{1,0:T(8,128)(2,1)S(1)} %get-tuple-element.58), channel_id=1, source_target_pairs={{0,2},{1,3},{2,0},{3,1},{4,6},{5,7},{6,4},{7,5},{8,10},{9,11},{10,... | collective-permute-start | bytes 3981320 | tf_op jit(solution)/shard_map/ppermute | solution.py:312
  969.2 44.9 %collective-permute-start.103 = (bf16[288,1152]{1,0:T(8,128)(2,1)S(1)}, bf16[288,1152]{1,0:T(8,128)(2,1)S(1)}, u32[]{:S(2)}, u32[]{:S(2)}) collective-permute-start(bf16[288,1152]{1,0:T(8,128)(2,1)S(1)} %dynamic-slice_bitcast_fusion.5), channel_id=1, source_target_pairs={{0,4},{4,0},{8,12},{12,8},{16,20},{20,16},{24,28},{28,24},{1,5},{5... | collective-permute-start | bytes 1990664 | tf_op jit(solution)/shard_map/ppermute | solution.py:312
  969.4 45.3 %collective-permute-start.109 = (bf16[288,1152]{1,0:T(8,128)(2,1)S(1)}, bf16[288,1152]{1,0:T(8,128)(2,1)S(1)}, u32[]{:S(2)}, u32[]{:S(2)}) collective-permute-start(bf16[288,1152]{1,0:T(8,128)(2,1)S(1)} %dynamic-slice_bitcast_fusion.4), channel_id=1, source_target_pairs={{0,8},{4,12},{8,0},{12,4},{16,24},{20,28},{24,16},{28,20},{1,9},{5... | collective-permute-start | bytes 1990664 | tf_op jit(solution)/shard_map/ppermute | solution.py:312
  (266 other events, 3565.9 us)
